TPU v7x, 32 devices: a whole 2x2x4 slice. The times are simulated.
32 devices in a mesh: dp: 8 (over z, x), mp: 4 (over y, core).
Axes of the slice: x: 2, y: 2, z: 4, core: 2. Of those that a mesh axis runs over, the one named last changes fastest.
Arguments:
- tokens: bfloat16 [8192, 2048], P('dp', 'mp'), may hold values from -6 to 6
- norm_gain: bfloat16 [2048], replicated, may hold values from 0.099609375 to 1.8984375
- wi_gate: bfloat16 [2048, 5120], P(None, 'mp'), may hold values from -0.125 to 0.125
- wi_linear: bfloat16 [2048, 5120], P(None, 'mp'), may hold values from -0.125 to 0.125
- wo_out: bfloat16 [5120, 2048], P('mp'), may hold values from -0.078125 to 0.078125
- task_table: float32 [8, 64], replicated, may hold values from -5 to 5
- layer_table: float32 [24, 64], replicated, may hold values from -5 to 5
- task_ids: int32 [64], P('dp'), may hold values from 0 to 7
- layer_index: int32 [1], replicated, may hold values from 0 to 23
- hyper_in: bfloat16 [128, 1024], P(None, 'mp'), may hold values from -0.5 to 0.5
- gen_down: bfloat16 [1024, 131072], P(None, ('mp', 'dp')), may hold values from -0.0078125 to 0.0078125
- gen_up: bfloat16 [1024, 131072], P(None, ('mp', 'dp')), may hold values from -0.046875 to 0.046875
Outputs:
- mixed: bfloat16 [8192, 2048], P('dp', 'mp')
All inputs are finite; a program needn't handle non-finite values.
Results may differ from a plain program's by a relative error of at most 0.019.
Values may be sent and summed in bfloat16 or wider, within the bound.
A program may use at most 128 MiB of HBM per device.

v0:
```python
import jax
import jax.numpy as jnp
from jax import lax
from jax.sharding import PartitionSpec as P

R = 64


def matmul(left, right):
    return jnp.dot(left, right, preferred_element_type=jnp.float32)


def per_device(
    tokens,
    norm_gain,
    wi_gate,
    wi_linear,
    wo_out,
    task_table,
    layer_table,
    task_ids,
    layer_index,
    hyper_in,
    gen_down,
    gen_up,
):
    task_count = task_table.shape[0]
    layer_row = jnp.take(layer_table, layer_index, axis=0)
    embed = jnp.concatenate(
        [task_table, jnp.broadcast_to(layer_row, (task_count, layer_row.shape[1]))], axis=1
    ).astype(jnp.bfloat16)
    hidden_part = jnp.maximum(matmul(embed, hyper_in), 0.0).astype(jnp.bfloat16)
    hidden = lax.all_gather(hidden_part, "mp", axis=1, tiled=True)
    every_id = lax.all_gather(task_ids, "dp", axis=0, tiled=True)
    wanted = jnp.take(hidden, every_id, axis=0)
    made = (
        matmul(wanted, gen_down).astype(jnp.bfloat16),
        matmul(wanted, gen_up).astype(jnp.bfloat16),
    )
    local_down, local_up = (
        lax.all_to_all(made[0], "dp", split_axis=0, concat_axis=1, tiled=True),
        lax.all_to_all(made[1], "dp", split_axis=0, concat_axis=1, tiled=True),
    )
    full_rows = lax.all_gather(tokens, "mp", axis=1, tiled=True)
    wide = full_rows.astype(jnp.float32)
    scale = lax.rsqrt(jnp.mean(wide * wide, axis=-1, keepdims=True) + 1e-06)
    normed = (wide * scale * norm_gain.astype(jnp.float32)).astype(jnp.bfloat16)
    gate = matmul(normed, wi_gate)
    linear = matmul(normed, wi_linear)
    act = (jax.nn.gelu(gate, approximate=True) * linear).astype(jnp.bfloat16)
    seqs_dev = task_ids.shape[0]
    tok_dev = tokens.shape[0]
    seq_len = tok_dev // seqs_dev
    partial_sums = matmul(act, wo_out)
    ffout = lax.psum_scatter(
        partial_sums.astype(jnp.bfloat16), "mp", scatter_dimension=1, tiled=True
    )
    down_block = local_down.reshape(seqs_dev, -1, R)
    up_block = local_up.reshape(seqs_dev, -1, R)
    blocks = ffout.reshape(seqs_dev, seq_len, -1)
    squeeze_part = jnp.einsum(
        "std,sdr->str", blocks, down_block, preferred_element_type=jnp.float32
    )
    squeeze_full = lax.psum(squeeze_part.astype(jnp.bfloat16), "mp").astype(jnp.float32)
    squeezed = jnp.maximum(squeeze_full, 0.0).astype(jnp.bfloat16)
    expand = jnp.einsum("str,sdr->std", squeezed, up_block, preferred_element_type=jnp.float32)
    total = tokens.astype(jnp.float32) + ffout.astype(jnp.float32) + expand.reshape(tok_dev, -1)
    return total.astype(jnp.bfloat16)


def solution(mesh):
    return jax.shard_map(
        per_device,
        mesh=mesh,
        in_specs=(
            P("dp", "mp"),
            P(),
            P(None, "mp"),
            P(None, "mp"),
            P("mp", None),
            P(),
            P(),
            P("dp"),
            P(),
            P(None, "mp"),
            P(None, ("mp", "dp")),
            P(None, ("mp", "dp")),
        ),
        out_specs=P("dp", "mp"),
        check_vma=False,
    )
```

profile of v0, /device:TPU:0, one launch (start us, length us, event | category | flops | bytes accessed | tf_op | source)
XLA Modules:
  0.0 174.6 jit_solution(7065484068272233757)
XLA Ops:
  6.5 0.7 all-gather.2.cloned.1.call-update
  7.3 0.7 convert_element_type.45
  8.0 38.1 %all-gather.2.cloned.1.call-done = bf16[1024,2048]{1,0:T(8,128)(2,1)} async-done(((bf16[1024,512]{1,0:T(8,128)(2,1)}), bf16[1024,2048]{1,0:T(8,128)(2,1)}) %all-gather.2.cloned.1.call-update) | async-done | bytes 4194320 | tf_op jit(solution)/shard_map/all_gather | solution.py:44
  46.1 3.1 %fusion = f32[1024]{0:T(1024)S(1)} fusion(bf16[1024,2048]{1,0:T(8,128)(2,1)} %all-gather.2.cloned.1.call-done), kind=kLoop, calls=%fused_computation.3 | loop fusion | flops 6290432 | bytes 4198400 | tf_op jit(solution)/shard_map/reduce_sum | solution.py:46
  49.2 10.7 %fusion.16 = f32[1024,1280]{1,0:T(8,128)} fusion(bf16[2048,1280]{1,0:T(8,128)(2,1)} %param.14, bf16[1024,2048]{1,0:T(8,128)(2,1)} %all-gather.2.cloned.1.call-done, f32[2048]{0:T(1024)S(1)} %convert_element_type.45, f32[1024]{0:T(1024)S(1)} %add_rsqrt_fusion), kind=kOutput, calls=%fused_computation.23 | convolution fusion | flops 5377097728 | bytes 14692352 | tf_op jit(solution)/shard_map/dot_general | solution.py:10
  59.9 19.9 %convolution_convert_fusion.2 = bf16[1024,2048]{1,0:T(8,128)(2,1)} fusion(bf16[1280,2048]{1,0:T(8,128)(2,1)} %param.16, f32[1024,1280]{1,0:T(8,128)} %fusion.16, bf16[2048,1280]{1,0:T(8,128)(2,1)} %param.15, bf16[1024,2048]{1,0:T(8,128)(2,1)} %all-gather.2.cloned.1.call-done, f32[2048]{0:T(1024)S(1)} %convert_element_type.45, f32[1024]{0:T(1024)S(1)} %add_rsqrt_fusion), kind=kOutput, calls=%fused_computation.20 | convolution fusion | flops 10761011200 | bytes 24129536 | tf_op jit(solution)/shard_map/dot_general | solution.py:10
  80.5 0.7 fusion.27
  81.3 0.6 dynamic-slice.4
  82.8 11.4 %all-reduce = s32[64]{0:T(128)S(1)} all-reduce(s32[64]{0:T(128)S(1)} %dynamic-update-slice.1), channel_id=1, replica_groups=mesh['dp'=8,'mp'=4] {'dp'}, use_global_device_ids=true, to_apply=%add | all-reduce | flops 64 | bytes 512
  94.3 5.2 %all_gather.11 = bf16[8,1024]{1,0:T(8,128)(2,1)S(1)} all-gather(bf16[8,256]{1,0:T(8,128)(2,1)S(1)} %fusion.18), channel_id=1, replica_groups=mesh['dp'=8,'mp'=4] {'mp'}, dimensions={1}, use_global_device_ids=true | all-gather | bytes 20480 | tf_op jit(solution)/shard_map/all_gather | solution.py:33
  99.5 0.7 gather_fusion
  100.2 5.8 %fusion.12 = bf16[8,8,4096]{2,1,0:T(8,128)(2,1)} fusion(bf16[1024,4096]{1,0:T(8,128)(2,1)} %param.22, bf16[64,1024]{1,0:T(8,128)(2,1)S(1)} %gather_fusion, pred[64]{0:T(512)(128)(4,1)S(1)} %compare_and_fusion), kind=kOutput, calls=%fused_computation.18 | convolution fusion | flops 537198592 | bytes 9044032 | tf_op jit(solution)/shard_map/dot_general | solution.py:10
  106.1 3.5 %all-to-all-start = ((bf16[8,8,4096]{2,1,0:T(8,128)(2,1)}), bf16[8,8,4096]{2,1,0:T(8,128)(2,1)S(1)}, u32[]{:S(2)}, u32[]{:S(2)}) async-start(bf16[8,8,4096]{2,1,0:T(8,128)(2,1)} %fusion.12), calls=%async_computation.1 | async-start | bytes 1048576 | tf_op jit(solution)/shard_map/all_to_all | solution.py:41
  109.6 5.8 %fusion.13 = bf16[8,8,4096]{2,1,0:T(8,128)(2,1)} fusion(bf16[1024,4096]{1,0:T(8,128)(2,1)} %param.23, bf16[64,1024]{1,0:T(8,128)(2,1)S(1)} %gather_fusion, pred[64]{0:T(512)(128)(4,1)S(1)} %compare_and_fusion), kind=kOutput, calls=%fused_computation.19 | convolution fusion | flops 537198592 | bytes 9044032 | tf_op jit(solution)/shard_map/dot_general | solution.py:10
  115.4 9.4 %all-to-all-done = bf16[8,8,4096]{2,1,0:T(8,128)(2,1)S(1)} async-done(((bf16[8,8,4096]{2,1,0:T(8,128)(2,1)}), bf16[8,8,4096]{2,1,0:T(8,128)(2,1)S(1)}, u32[]{:S(2)}, u32[]{:S(2)}) %all-to-all-start) | async-done | bytes 524320 | tf_op jit(solution)/shard_map/all_to_all | solution.py:41
  124.8 4.3 %all-to-all-start.1 = ((bf16[8,8,4096]{2,1,0:T(8,128)(2,1)}), bf16[8,8,4096]{2,1,0:T(8,128)(2,1)}, u32[]{:S(2)}, u32[]{:S(2)}) async-start(bf16[8,8,4096]{2,1,0:T(8,128)(2,1)} %fusion.13), calls=%async_computation.2 | async-start | bytes 1048576 | tf_op jit(solution)/shard_map/all_to_all | solution.py:42
  129.4 1.1 reshape.46
  130.6 2.5 %convolution_convert_fusion.3 = bf16[8,128,64]{1,2,0:T(8,128)(2,1)} fusion(bf16[8,128,512]{2,1,0:T(8,128)(2,1)} %bitcast.25, bf16[8,512,64]{2,1,0:T(8,128)(2,1)S(1)} %reshape.46), kind=kOutput, calls=%fused_computation.24 | convolution fusion | flops 67174400 | bytes 1703936 | tf_op jit(solution)/shard_map/std,sdr->str/dot_general | solution.py:61
  133.1 10.2 %all-to-all-done.1 = bf16[8,8,4096]{2,1,0:T(8,128)(2,1)} async-done(((bf16[8,8,4096]{2,1,0:T(8,128)(2,1)}), bf16[8,8,4096]{2,1,0:T(8,128)(2,1)}, u32[]{:S(2)}, u32[]{:S(2)}) %all-to-all-start.1) | async-done | bytes 524320 | tf_op jit(solution)/shard_map/all_to_all | solution.py:42
  143.3 2.1 %copy.18 = bf16[8,8,4096]{2,1,0:T(8,128)(2,1)} copy(bf16[8,8,4096]{2,0,1:T(8,128)(2,1)} %bitcast.8) | data formatting | bytes 1048576 | tf_op jit(solution)/shard_map/all_to_all | solution.py:42
  145.4 2.1 %reshape.47 = bf16[8,512,64]{2,1,0:T(8,128)(2,1)S(1)} reshape(bf16[8,8,4096]{2,1,0:T(8,128)(2,1)} %copy.18) | data formatting | bytes 1048576 | tf_op jit(solution)/shard_map/reshape | solution.py:59
  147.5 17.7 %all-reduce.3.cloned.1.call-done = bf16[8,128,64]{1,2,0:T(8,128)(2,1)} async-done(((bf16[8,128,64]{1,2,0:T(8,128)(2,1)}), bf16[8,128,64]{1,2,0:T(8,128)(2,1)}) %all-reduce.3.cloned.1.call-update) | async-done | bytes 131088 | tf_op jit(solution)/shard_map/psum | solution.py:64
  165.2 1.4 fusion.21
  166.6 1.4 fusion.14
  (28 shorter events, 0.9 us)
Async XLA Ops:
  6.5 87.6 %copy-start = (bf16[128,256]{1,0:T(8,128)(2,1)S(1)}, bf16[128,256]{1,0:T(8,128)(2,1)}, u32[]{:S(2)}) copy-start(bf16[128,256]{1,0:T(8,128)(2,1)} %param.21) | copy-start | bytes 196612
  6.5 39.6 %all-gather.2.cloned.1.call-start = ((), (), s32[]{:S(2)}) async-start(), calls=%async_computation.3 | async-start | bytes 5242880 | tf_op jit(solution)/shard_map/all_gather | solution.py:44
  7.3 123.3 %reduce-scatter.2.cloned.1.call-start = ((), (), s32[]{:S(2)}) async-start(), calls=%async_computation.4 | async-start | bytes 5242880 | tf_op jit(solution)/shard_map/reduce_scatter | solution.py:55
  59.9 20.6 %copy-start.3 = (f32[8,64]{1,0:T(8,128)S(1)}, f32[8,64]{1,0:T(8,128)}, u32[]{:S(2)}) copy-start(f32[8,64]{1,0:T(8,128)} %param.17) | copy-start | bytes 6148
  59.9 21.4 %copy-start.5 = (u32[32]{0:T(128)S(1)}, u32[32]{0:T(128)}, u32[]{:S(2)}) copy-start(u32[32]{0:T(128)} %constant.73) | copy-start | bytes 388
  59.9 22.7 %copy-start.4 = (s32[8]{0:T(128)S(1)}, s32[8]{0:T(128)}, u32[]{:S(2)}) copy-start(s32[8]{0:T(128)} %param.19) | copy-start | bytes 100
  106.1 18.7 %all-to-all-start = ((bf16[8,8,4096]{2,1,0:T(8,128)(2,1)}), bf16[8,8,4096]{2,1,0:T(8,128)(2,1)S(1)}, u32[]{:S(2)}, u32[]{:S(2)}) async-start(bf16[8,8,4096]{2,1,0:T(8,128)(2,1)} %fusion.12), calls=%async_computation.1 | async-start | bytes 1048576 | tf_op jit(solution)/shard_map/all_to_all | solution.py:41
  124.8 18.6 %all-to-all-start.1 = ((bf16[8,8,4096]{2,1,0:T(8,128)(2,1)}), bf16[8,8,4096]{2,1,0:T(8,128)(2,1)}, u32[]{:S(2)}, u32[]{:S(2)}) async-start(bf16[8,8,4096]{2,1,0:T(8,128)(2,1)} %fusion.13), calls=%async_computation.2 | async-start | bytes 1048576 | tf_op jit(solution)/shard_map/all_to_all | solution.py:42
  129.1 36.1 %all-reduce.3.cloned.1.call-start = ((), (), s32[]{:S(2)}) async-start(), calls=%async_computation.5 | async-start | bytes 262144 | tf_op jit(solution)/shard_map/psum | solution.py:64
  129.1 37.5 %copy-start.1 = (bf16[1024,512]{1,0:T(8,128)(2,1)S(1)}, bf16[1024,512]{1,0:T(8,128)(2,1)}, u32[]{:S(2)}) copy-start(bf16[1024,512]{1,0:T(8,128)(2,1)} %param.12) | copy-start | bytes 3145732
  130.6 36.0 %copy-start.2 = (bf16[1024,512]{1,0:T(8,128)(2,1)S(1)}, bf16[1024,512]{1,0:T(8,128)(2,1)}, u32[]{:S(2)}) copy-start(bf16[1024,512]{1,0:T(8,128)(2,1)} %reduce-scatter.2.cloned.1.call-done) | copy-start | bytes 3145732
Sparse Core Ops, SparseCore 0:
  8.9 37.1 all-gather.1
  80.0 44.3 reduce-scatter.1
  133.2 31.9 all-reduce.2
where the time goes:
time: 175 us
  waiting for transfers between devices  76.2 us (44%)
  matrix products  46.2 us (26%)
  blocking collectives  16.6 us (9%)
  between operations  14.6 us (8%)
  starting transfers between devices  7.9 us (5%)
  local copies, waits for them, and re-layouts  7.23 us (4%)
  other arithmetic  5.92 us (3%)
    dot_general x5, matrix products, matmul(): return jnp.dot(left, right, preferred_element_type=jnp.float32)  42.4 us
    all_gather x1, waiting for transfers between devices, per_device(): full_rows = lax.all_gather(tokens, 'mp', axis=1, tiled=True)  38.1 us
    psum x1, waiting for transfers between devices, per_device(): lax.psum(squeeze_part.astype(jnp.bfloat16), 'mp').astype(jnp.float32)  17.7 us
    unnamed x1, blocking collectives  11.4 us
    all_to_all x1, waiting for transfers between devices, per_device(): lax.all_to_all(made[1], 'dp', split_axis=0, concat_axis=1, tiled=True)  10.2 us
    all_to_all x1, waiting for transfers between devices, per_device(): lax.all_to_all(made[0], 'dp', split_axis=0, concat_axis=1, tiled=True)  9.39 us
    all_gather x1, blocking collectives, per_device(): hidden = lax.all_gather(hidden_part, 'mp', axis=1, tiled=True)  5.2 us
    all_to_all x1, starting transfers between devices, per_device(): lax.all_to_all(made[1], 'dp', split_axis=0, concat_axis=1, tiled=True)  4.33 us
  transfers between devices with their start and end apart: 5, of which 4 were waited for; matrix products, arithmetic and copies ran while one was open for 13% of the time, Pallas kernels for 0%

commit v1 on v0

--- a/solution.py
+++ b/solution.py
@@ -61,7 +61,9 @@
     squeeze_part = jnp.einsum(
         "std,sdr->str", blocks, down_block, preferred_element_type=jnp.float32
     )
-    squeeze_full = lax.psum(squeeze_part.astype(jnp.bfloat16), "mp").astype(jnp.float32)
+    squeeze_full = jnp.sum(lax.all_gather(squeeze_part.astype(jnp.bfloat16), "mp"), axis=0).astype(
+        jnp.float32
+    )
     squeezed = jnp.maximum(squeeze_full, 0.0).astype(jnp.bfloat16)
     expand = jnp.einsum("str,sdr->std", squeezed, up_block, preferred_element_type=jnp.float32)
     total = tokens.astype(jnp.float32) + ffout.astype(jnp.float32) + expand.reshape(tok_dev, -1)

time: 175 us -> 164 us (0.937)
  waiting for transfers between devices: 76.2 us -> 60.5 us
  blocking collectives: 16.6 us -> 23.5 us
  local copies, waits for them, and re-layouts: 7.23 us -> 5.43 us
    psum x1 -> x0, waiting for transfers between devices: 17.7 us -> none  [per_device(): lax.psum(squeeze_part.astype(jnp.bfloat16), 'mp').astype(jnp.float32)]
    all_gather x0 -> x1, blocking collectives: none -> 6.95 us  [per_device(): lax.all_gather(squeeze_part.astype(jnp.bfloat16), 'mp')]
    all_to_all x1, waiting for transfers between devices: 10.2 us -> 12.2 us  [per_device(): lax.all_to_all(made[1], 'dp', split_axis=0, concat_axis=1, tiled=True)]
    all_to_all x1, local copies, waits for them, and re-layouts: 2.13 us -> 0.29 us  [per_device(): lax.all_to_all(made[1], 'dp', split_axis=0, concat_axis=1, tiled=True)]
  transfers between devices with their start and end apart: 5 -> 4, of which waited for: 4 -> 3; matrix products, arithmetic and copies ran while one was open for 13% -> 11% of each run, Pallas kernels for 0% -> 0%
where the time goes in v1:
time: 164 us
  waiting for transfers between devices  60.5 us (37%)
  matrix products  45 us (27%)
  blocking collectives  23.5 us (14%)
  between operations  14.9 us (9%)
  starting transfers between devices  7.21 us (4%)
  other arithmetic  7.04 us (4%)
  local copies, waits for them, and re-layouts  5.43 us (3%)
    dot_general x5, matrix products, matmul(): return jnp.dot(left, right, preferred_element_type=jnp.float32)  42.4 us
    all_gather x1, waiting for transfers between devices, per_device(): full_rows = lax.all_gather(tokens, 'mp', axis=1, tiled=True)  38.1 us
    all_to_all x1, waiting for transfers between devices, per_device(): lax.all_to_all(made[1], 'dp', split_axis=0, concat_axis=1, tiled=True)  12.2 us
    unnamed x1, blocking collectives  11.3 us
    all_to_all x1, waiting for transfers between devices, per_device(): lax.all_to_all(made[0], 'dp', split_axis=0, concat_axis=1, tiled=True)  9.37 us
    all_gather x1, blocking collectives, per_device(): lax.all_gather(squeeze_part.astype(jnp.bfloat16), 'mp')  6.95 us
    all_gather x1, blocking collectives, per_device(): hidden = lax.all_gather(hidden_part, 'mp', axis=1, tiled=True)  5.2 us
    all_to_all x1, starting transfers between devices, per_device(): lax.all_to_all(made[1], 'dp', split_axis=0, concat_axis=1, tiled=True)  3.67 us
  transfers between devices with their start and end apart: 4, of which 3 were waited for; matrix products, arithmetic and copies ran while one was open for 11% of the time, Pallas kernels for 0%

profile of v1, /device:TPU:0, one launch (start us, length us, event | category | flops | bytes accessed | tf_op | source)
XLA Modules:
  0.0 163.5 jit_solution(2229031257675506405)
XLA Ops:
  6.5 0.7 all-gather.3.cloned.1.call-update
  7.3 0.7 convert_element_type.47
  8.0 38.1 %all-gather.3.cloned.1.call-done = bf16[1024,2048]{1,0:T(8,128)(2,1)} async-done(((bf16[1024,512]{1,0:T(8,128)(2,1)}), bf16[1024,2048]{1,0:T(8,128)(2,1)}) %all-gather.3.cloned.1.call-update) | async-done | bytes 4194320 | tf_op jit(solution)/shard_map/all_gather | solution.py:44
  46.1 3.1 %fusion = f32[1024]{0:T(1024)S(1)} fusion(bf16[1024,2048]{1,0:T(8,128)(2,1)} %all-gather.3.cloned.1.call-done), kind=kLoop, calls=%fused_computation.3 | loop fusion | flops 6290432 | bytes 4198400 | tf_op jit(solution)/shard_map/reduce_sum | solution.py:46
  49.2 10.7 %fusion.16 = f32[1024,1280]{1,0:T(8,128)} fusion(bf16[2048,1280]{1,0:T(8,128)(2,1)} %param.14, bf16[1024,2048]{1,0:T(8,128)(2,1)} %all-gather.3.cloned.1.call-done, f32[2048]{0:T(1024)S(1)} %convert_element_type.47, f32[1024]{0:T(1024)S(1)} %add_rsqrt_fusion), kind=kOutput, calls=%fused_computation.23 | convolution fusion | flops 5377097728 | bytes 14692352 | tf_op jit(solution)/shard_map/dot_general | solution.py:10
  59.9 19.9 %convolution_convert_fusion.2 = bf16[1024,2048]{1,0:T(8,128)(2,1)} fusion(bf16[1280,2048]{1,0:T(8,128)(2,1)} %param.16, f32[1024,1280]{1,0:T(8,128)} %fusion.16, bf16[2048,1280]{1,0:T(8,128)(2,1)} %param.15, bf16[1024,2048]{1,0:T(8,128)(2,1)} %all-gather.3.cloned.1.call-done, f32[2048]{0:T(1024)S(1)} %convert_element_type.47, f32[1024]{0:T(1024)S(1)} %add_rsqrt_fusion), kind=kOutput, calls=%fused_computation.20 | convolution fusion | flops 10761011200 | bytes 24129536 | tf_op jit(solution)/shard_map/dot_general | solution.py:10
  80.5 0.7 fusion.27
  81.3 0.6 dynamic-slice.4
  82.8 11.3 %all-reduce = s32[64]{0:T(128)S(1)} all-reduce(s32[64]{0:T(128)S(1)} %dynamic-update-slice.1), channel_id=1, replica_groups=mesh['dp'=8,'mp'=4] {'dp'}, use_global_device_ids=true, to_apply=%add | all-reduce | flops 64 | bytes 512
  94.3 5.2 %all_gather.17 = bf16[8,1024]{1,0:T(8,128)(2,1)S(1)} all-gather(bf16[8,256]{1,0:T(8,128)(2,1)S(1)} %fusion.18), channel_id=1, replica_groups=mesh['dp'=8,'mp'=4] {'mp'}, dimensions={1}, use_global_device_ids=true | all-gather | bytes 20480 | tf_op jit(solution)/shard_map/all_gather | solution.py:33
  99.5 0.7 gather_fusion
  100.2 5.8 %fusion.12 = bf16[8,8,4096]{2,1,0:T(8,128)(2,1)} fusion(bf16[1024,4096]{1,0:T(8,128)(2,1)} %param.22, bf16[64,1024]{1,0:T(8,128)(2,1)S(1)} %gather_fusion, pred[64]{0:T(512)(128)(4,1)S(1)} %compare_and_fusion), kind=kOutput, calls=%fused_computation.18 | convolution fusion | flops 537198592 | bytes 9044032 | tf_op jit(solution)/shard_map/dot_general | solution.py:10
  106.0 3.5 %all-to-all-start = ((bf16[8,8,4096]{2,1,0:T(8,128)(2,1)}), bf16[8,8,4096]{2,1,0:T(8,128)(2,1)S(1)}, u32[]{:S(2)}, u32[]{:S(2)}) async-start(bf16[8,8,4096]{2,1,0:T(8,128)(2,1)} %fusion.12), calls=%async_computation.1 | async-start | bytes 1048576 | tf_op jit(solution)/shard_map/all_to_all | solution.py:41
  109.5 5.8 %fusion.13 = bf16[8,8,4096]{2,1,0:T(8,128)(2,1)} fusion(bf16[1024,4096]{1,0:T(8,128)(2,1)} %param.23, bf16[64,1024]{1,0:T(8,128)(2,1)S(1)} %gather_fusion, pred[64]{0:T(512)(128)(4,1)S(1)} %compare_and_fusion), kind=kOutput, calls=%fused_computation.19 | convolution fusion | flops 537198592 | bytes 9044032 | tf_op jit(solution)/shard_map/dot_general | solution.py:10
  115.3 9.4 %all-to-all-done = bf16[8,8,4096]{2,1,0:T(8,128)(2,1)S(1)} async-done(((bf16[8,8,4096]{2,1,0:T(8,128)(2,1)}), bf16[8,8,4096]{2,1,0:T(8,128)(2,1)S(1)}, u32[]{:S(2)}, u32[]{:S(2)}) %all-to-all-start) | async-done | bytes 524320 | tf_op jit(solution)/shard_map/all_to_all | solution.py:41
  124.7 3.7 %all-to-all-start.1 = ((bf16[8,8,4096]{2,1,0:T(8,128)(2,1)}), bf16[8,8,4096]{2,1,0:T(8,128)(2,1)S(1)}, u32[]{:S(2)}, u32[]{:S(2)}) async-start(bf16[8,8,4096]{2,1,0:T(8,128)(2,1)} %fusion.13), calls=%async_computation.2 | async-start | bytes 1048576 | tf_op jit(solution)/shard_map/all_to_all | solution.py:42
  128.7 2.1 %reshape.46 = bf16[8,512,64]{2,1,0:T(8,128)(2,1)} reshape(bf16[8,8,4096]{2,1,0:T(8,128)(2,1)S(1)} %copy.17) | data formatting | bytes 1048576 | tf_op jit(solution)/shard_map/reshape | solution.py:58
  130.8 12.2 %all-to-all-done.1 = bf16[8,8,4096]{2,1,0:T(8,128)(2,1)S(1)} async-done(((bf16[8,8,4096]{2,1,0:T(8,128)(2,1)}), bf16[8,8,4096]{2,1,0:T(8,128)(2,1)S(1)}, u32[]{:S(2)}, u32[]{:S(2)}) %all-to-all-start.1) | async-done | bytes 524320 | tf_op jit(solution)/shard_map/all_to_all | solution.py:42
  143.3 1.1 reshape.47
  144.5 2.1 %convolution_convert_fusion.3 = bf16[8,128,64]{1,2,0:T(8,128)(2,1)S(1)} fusion(bf16[8,128,512]{2,1,0:T(8,128)(2,1)} %bitcast.26, bf16[8,512,64]{2,1,0:T(8,128)(2,1)} %reshape.46), kind=kOutput, calls=%fused_computation.24 | convolution fusion | flops 67174400 | bytes 1703936 | tf_op jit(solution)/shard_map/std,sdr->str/dot_general | solution.py:61
  146.7 7.0 %all-gather = bf16[32,128,64]{1,2,0:T(8,128)(2,1)} all-gather(bf16[8,128,64]{1,2,0:T(8,128)(2,1)S(1)} %convolution_convert_fusion.3), channel_id=2, replica_groups=mesh['dp'=8,'mp'=4] {'mp'}, dimensions={0}, use_global_device_ids=true | all-gather | bytes 655360 | tf_op jit(solution)/shard_map/all_gather | solution.py:64
  153.6 1.1 reduce_sum.22
  154.7 0.5 fusion.21
  155.3 1.4 fusion.14
  (27 shorter events, 1.2 us)
Async XLA Ops:
  6.5 87.6 %copy-start = (bf16[128,256]{1,0:T(8,128)(2,1)S(1)}, bf16[128,256]{1,0:T(8,128)(2,1)}, u32[]{:S(2)}) copy-start(bf16[128,256]{1,0:T(8,128)(2,1)} %param.21) | copy-start | bytes 196612
  6.5 39.6 %all-gather.3.cloned.1.call-start = ((), (), s32[]{:S(2)}) async-start(), calls=%async_computation.3 | async-start | bytes 5242880 | tf_op jit(solution)/shard_map/all_gather | solution.py:44
  7.3 137.2 %reduce-scatter.2.cloned.1.call-start = ((), (), s32[]{:S(2)}) async-start(), calls=%async_computation.4 | async-start | bytes 5242880 | tf_op jit(solution)/shard_map/reduce_scatter | solution.py:55
  59.9 20.6 %copy-start.3 = (f32[8,64]{1,0:T(8,128)S(1)}, f32[8,64]{1,0:T(8,128)}, u32[]{:S(2)}) copy-start(f32[8,64]{1,0:T(8,128)} %param.17) | copy-start | bytes 6148
  59.9 21.4 %copy-start.5 = (u32[32]{0:T(128)S(1)}, u32[32]{0:T(128)}, u32[]{:S(2)}) copy-start(u32[32]{0:T(128)} %constant.75) | copy-start | bytes 388
  59.9 22.7 %copy-start.4 = (s32[8]{0:T(128)S(1)}, s32[8]{0:T(128)}, u32[]{:S(2)}) copy-start(s32[8]{0:T(128)} %param.19) | copy-start | bytes 100
  106.0 18.7 %all-to-all-start = ((bf16[8,8,4096]{2,1,0:T(8,128)(2,1)}), bf16[8,8,4096]{2,1,0:T(8,128)(2,1)S(1)}, u32[]{:S(2)}, u32[]{:S(2)}) async-start(bf16[8,8,4096]{2,1,0:T(8,128)(2,1)} %fusion.12), calls=%async_computation.1 | async-start | bytes 1048576 | tf_op jit(solution)/shard_map/all_to_all | solution.py:41
  124.7 18.3 %all-to-all-start.1 = ((bf16[8,8,4096]{2,1,0:T(8,128)(2,1)}), bf16[8,8,4096]{2,1,0:T(8,128)(2,1)S(1)}, u32[]{:S(2)}, u32[]{:S(2)}) async-start(bf16[8,8,4096]{2,1,0:T(8,128)(2,1)} %fusion.13), calls=%async_computation.2 | async-start | bytes 1048576 | tf_op jit(solution)/shard_map/all_to_all | solution.py:42
  128.7 26.5 %copy-start.1 = (bf16[1024,512]{1,0:T(8,128)(2,1)S(1)}, bf16[1024,512]{1,0:T(8,128)(2,1)}, u32[]{:S(2)}) copy-start(bf16[1024,512]{1,0:T(8,128)(2,1)} %param.12) | copy-start | bytes 3145732
  144.5 10.7 %copy-start.2 = (bf16[1024,512]{1,0:T(8,128)(2,1)S(1)}, bf16[1024,512]{1,0:T(8,128)(2,1)}, u32[]{:S(2)}) copy-start(bf16[1024,512]{1,0:T(8,128)(2,1)} %reduce-scatter.2.cloned.1.call-done) | copy-start | bytes 3145732
Sparse Core Ops, SparseCore 0:
  8.9 37.1 all-gather.2
  80.0 44.3 reduce-scatter.1
